TPU v7x, 512 devices: a whole 4x8x8 slice. The times are simulated.
512 devices in a mesh: obs: 64 (over z_hi, x, y), head: 8 (over z_lo, core).
Axes of the slice: x: 4, y: 8, z: 8 (z_hi: 2, z_lo: 4; z = z_hi * 4 + z_lo), core: 2. Of those that a mesh axis runs over, the one named last changes fastest.
Arguments:
- queries: bfloat16 [1024, 2048], P('obs', 'head'), may hold values from -6 to 6
- out_grad: bfloat16 [1024, 2048], P('obs', 'head'), may hold values from -6 to 6
- attn_out: bfloat16 [1024, 2048], P('obs', 'head'), may hold values from -6 to 6
- logsumexp: float32 [1024, 16], P('obs', 'head'), may hold values from 2.5 to 4.5
- keys: bfloat16 [24576, 2048], P('obs', 'head'), may hold values from -6 to 6
- values: bfloat16 [24576, 2048], P('obs', 'head'), may hold values from -6 to 6
- obs_counts: int32 [64], P('obs'), may hold values from 1 to 384, as said below
- query_weight: bfloat16 [2048, 2048], P(None, 'head'), may hold values from -0.125 to 0.125
Outputs:
- key_grad: bfloat16 [24576, 2048], P('obs', 'head')
- value_grad: bfloat16 [24576, 2048], P('obs', 'head')
- query_grad: bfloat16 [1024, 2048], P('obs', 'head')
- grid_grad: bfloat16 [1024, 2048], P('obs', 'head')
Inputs may be any that keep to these rules, and one draw needn't show every extreme that they name: Each index of obs holds its tokens in its first obs_counts slots of 384; in every draw some index is full, with exactly 384.
All inputs are finite; a program needn't handle non-finite values.
Results may differ from a plain program's by a relative error of at most 0.0055.
Values may be sent and summed in bfloat16 or wider, within the bound.
A program may use at most 64 MiB of HBM per device.

v0:
```python
import math

import jax
import jax.numpy as jnp
from jax import lax
from jax.sharding import PartitionSpec as P

DH = 128


def side_by_side(arrays, axis, dim, along):
    both = jnp.concatenate(arrays, axis=along)
    filled, at, outs = (lax.all_gather(both, axis, axis=dim, tiled=True), 0, [])
    for a in arrays:
        outs.append(lax.slice_in_dim(filled, at, at + a.shape[along], axis=along))
        at += a.shape[along]
    return tuple(outs)


def in_blocks(shard, dim, peers):
    before, after = (shard.shape[:dim], shard.shape[dim + 1 :])
    return jnp.moveaxis(shard.reshape(*before, peers, -1, *after), dim, 0)


def sent_and_summed(shard, axis, dim):
    tiles = in_blocks(shard, dim, lax.axis_size(axis))
    arrived = lax.all_to_all(tiles, axis, split_axis=0, concat_axis=0, tiled=True)
    return arrived.sum(axis=0)


def row_split(row_total):
    block_rows = row_total
    while block_rows > 512 and block_rows % 2 == 0:
        block_rows = block_rows // 2
    return (block_rows, row_total // block_rows)


def adjoint(query_rows, grad_rows, lse_rows, delta_rows, key_heads, value_heads, key_live):
    block_rows = query_rows.shape[0]
    heads_here = key_heads.shape[1]
    softmax_scale = 1.0 / math.sqrt(DH)
    query_heads = query_rows.reshape(block_rows, heads_here, DH)
    grad_heads = grad_rows.reshape(block_rows, heads_here, DH)
    scores = (
        jnp.einsum("qhd,khd->hqk", query_heads, key_heads, preferred_element_type=jnp.float32)
        * softmax_scale
    )
    probs = jnp.exp(scores - lse_rows.T[:, :, None]) * key_live[None, None, :]
    dprobs = jnp.einsum("qhd,khd->hqk", grad_heads, value_heads, preferred_element_type=jnp.float32)
    dscores = (probs * (dprobs - delta_rows.T[:, :, None])).astype(jnp.bfloat16)
    return (probs.astype(jnp.bfloat16), dscores, query_heads, grad_heads)


def on_device(queries, out_grad, attn_out, logsumexp, keys, values, obs_counts, query_weight):
    softmax_scale = 1.0 / math.sqrt(DH)
    local_tokens = keys.shape[0]
    col_width = keys.shape[1]
    heads_here = col_width // DH
    own_rows = queries.shape[0]
    key_heads = keys.reshape(local_tokens, heads_here, DH)
    value_heads = values.reshape(local_tokens, heads_here, DH)
    key_live = (jnp.arange(local_tokens, dtype=jnp.int32) < obs_counts[0]).astype(jnp.float32)
    deltas = jnp.sum(
        out_grad.astype(jnp.float32).reshape(own_rows, heads_here, DH)
        * attn_out.astype(jnp.float32).reshape(own_rows, heads_here, DH),
        axis=2,
    )
    lse_all, delta_all = side_by_side((logsumexp, deltas), "obs", 0, 1)
    all_rows = lse_all.shape[0]
    zeros_tok = jnp.zeros((local_tokens, col_width), jnp.float32)
    start_totals = (zeros_tok, zeros_tok, jnp.zeros((all_rows, col_width), jnp.float32))
    pieces = side_by_side((queries, out_grad), "obs", 0, 1)
    query_part = pieces[0]
    grad_part = pieces[1]
    block_rows, step_total = row_split(query_part.shape[0])

    def visit_rows(step_index, running):
        offset = step_index * block_rows
        query_rows = lax.dynamic_slice_in_dim(query_part, offset, block_rows, 0)
        grad_rows = lax.dynamic_slice_in_dim(grad_part, offset, block_rows, 0)
        lse_rows = lax.dynamic_slice_in_dim(lse_all, offset, block_rows, 0)
        delta_rows = lax.dynamic_slice_in_dim(delta_all, offset, block_rows, 0)
        prob_half, dscores, query_heads, grad_heads = adjoint(
            query_rows, grad_rows, lse_rows, delta_rows, key_heads, value_heads, key_live
        )
        value_acc = running[1] + jnp.einsum(
            "hqk,qhd->khd", prob_half, grad_heads, preferred_element_type=jnp.float32
        ).reshape(local_tokens, col_width)
        key_acc = running[0] + softmax_scale * jnp.einsum(
            "hqk,qhd->khd", dscores, query_heads, preferred_element_type=jnp.float32
        ).reshape(local_tokens, col_width)
        query_part_grad = softmax_scale * jnp.einsum(
            "hqk,khd->qhd", dscores, key_heads, preferred_element_type=jnp.float32
        ).reshape(block_rows, col_width)
        return (
            key_acc,
            value_acc,
            lax.dynamic_update_slice_in_dim(running[2], query_part_grad, offset, 0),
        )

    key_acc, value_acc, query_full = lax.fori_loop(0, step_total, visit_rows, start_totals)
    query_sum = sent_and_summed(query_full, "obs", 0)
    query_half = query_sum.astype(jnp.bfloat16)
    partial_grid = jnp.einsum(
        "qc,dc->qd", query_half, query_weight, preferred_element_type=jnp.float32
    )
    grid_grad = sent_and_summed(partial_grid, "head", 1).astype(jnp.bfloat16)
    return (key_acc.astype(jnp.bfloat16), value_acc.astype(jnp.bfloat16), query_half, grid_grad)


def solution(mesh):
    in_specs = (
        P("obs", "head"),
        P("obs", "head"),
        P("obs", "head"),
        P("obs", "head"),
        P("obs", "head"),
        P("obs", "head"),
        P("obs"),
        P(None, "head"),
    )
    out_specs = (P("obs", "head"), P("obs", "head"), P("obs", "head"), P("obs", "head"))
    return jax.shard_map(
        on_device, mesh=mesh, in_specs=in_specs, out_specs=out_specs, check_vma=False
    )
```

profile of v0, /device:TPU:1, one launch (start us, length us, event | category | flops | bytes accessed | tf_op | source)
XLA Modules:
  0.0 303.2 jit_solution(114066415066632099)
XLA Ops:
  7.2 1.4 pad_maximum_fusion
  8.7 0.7 convert_multiply_fusion
  9.6 0.7 maximum_bitcast_fusion
  10.3 200.3 %all-gather = f32[64,16,4]{1,2,0:T(4,128)S(1)} all-gather(f32[1,16,4]{1,2,0:T(4,128)S(1)} %maximum_bitcast_fusion), channel_id=1, replica_groups=mesh['obs'=64,'head'=8] {'obs'}, dimensions={0}, use_global_device_ids=true | all-gather | bytes 16640 | tf_op jit(solution)/shard_map/all_gather | solution.py:13
  210.7 1.1 copy.48
  211.8 1.1 copy.51
  213.1 2.3 fusion.5
  215.4 1.0 broadcast_in_dim.16.clone
  216.4 12.2 %while.18 = (s32[]{:T(128)}, f32[384,256]{0,1:T(8,128)S(1)}, f32[384,256]{0,1:T(8,128)S(1)}, f32[1024,256]{1,0:T(8,128)}, bf16[1024,256]{1,0:T(8,128)(2,1)}, /*i...) while((s32[]{:T(128)}, f32[384,256]{0,1:T(8,128)S(1)}, ...), condition=%wide.region_2.0_spmd.clone, body=%wide.region_1.0_spmd.clone.sunk | while | flops 506692352 | bytes 16608485 | solution.py:101
  216.4 0.6 fusion.41
  217.1 1.0 constant_dynamic-slice_fusion.4
  218.2 1.0 constant_dynamic-slice_fusion.5
  219.4 0.5 exponential_multiply_fusion.2
  220.1 0.4 multiply_convert_fusion.2
  220.9 0.4 convolution_multiply_fusion.5
  221.7 0.8 constant_dynamic-update-slice_fusion.2
  222.5 0.6 fusion.41
  223.2 1.0 constant_dynamic-slice_fusion.4
  224.3 1.0 constant_dynamic-slice_fusion.5
  225.4 0.5 exponential_multiply_fusion.2
  226.2 0.4 multiply_convert_fusion.2
  226.7 0.3 convolution_multiply_fusion.4
  227.0 0.4 convolution_multiply_fusion.5
  227.8 0.8 constant_dynamic-update-slice_fusion.2
  228.6 26.2 %all_to_all.10 = f32[64,16,256]{2,1,0:T(8,128)S(1)} all-to-all(f32[64,16,256]{2,1,0:T(8,128)} %bitcast.79), channel_id=1, replica_groups=mesh['obs'=64,'head'=8] {'obs'}, dimensions={0} | all-to-all | bytes 2097152 | tf_op jit(solution)/shard_map/all_to_all | solution.py:27
  254.9 0.4 fusion.7
  255.3 0.7 copy.71
  255.9 34.0 %all-to-all-start.1 = ((f32[8,16,256]{2,1,0:T(8,128)}), f32[8,16,256]{2,1,0:T(8,128)S(1)}, u32[]{:S(2)}, u32[]{:S(2)}) async-start(f32[8,16,256]{2,1,0:T(8,128)} %bitcast.42), calls=%async_computation.1 | async-start | bytes 262144 | tf_op jit(solution)/shard_map/all_to_all | solution.py:27
  289.9 0.8 copy.55
  290.7 0.8 copy.56
  291.5 4.2 %all-to-all-done.1 = f32[8,16,256]{2,1,0:T(8,128)S(1)} async-done(((f32[8,16,256]{2,1,0:T(8,128)}), f32[8,16,256]{2,1,0:T(8,128)S(1)}, u32[]{:S(2)}, u32[]{:S(2)}) %all-to-all-start.1) | async-done | bytes 131104 | tf_op jit(solution)/shard_map/all_to_all | solution.py:27
  295.7 0.6 reduce_sum.29
  (32 shorter events, 2.9 us)
Async XLA Ops:
  7.2 247.7 %copy-start = (bf16[2048,256]{1,0:T(8,128)(2,1)S(1)}, bf16[2048,256]{1,0:T(8,128)(2,1)}, u32[]{:S(2)}) copy-start(bf16[2048,256]{1,0:T(8,128)(2,1)} %param.17) | copy-start | bytes 3145732
  7.2 205.9 %all-gather.3.cloned.1.call-start = ((), (), s32[]{:S(2)}) async-start(), calls=%async_computation.2 | async-start | bytes 1064960 | tf_op jit(solution)/shard_map/all_gather | solution.py:13
  254.9 41.4 %copy-start.1 = (bf16[16,256]{1,0:T(8,128)(2,1)}, bf16[16,256]{1,0:T(8,128)(2,1)S(1)}, u32[]{:S(2)}) copy-start(bf16[16,256]{1,0:T(8,128)(2,1)S(1)} %reduce_sum.28) | copy-start | bytes 24580
  255.9 39.7 %all-to-all-start.1 = ((f32[8,16,256]{2,1,0:T(8,128)}), f32[8,16,256]{2,1,0:T(8,128)S(1)}, u32[]{:S(2)}, u32[]{:S(2)}) async-start(f32[8,16,256]{2,1,0:T(8,128)} %bitcast.42), calls=%async_computation.1 | async-start | bytes 262144 | tf_op jit(solution)/shard_map/all_to_all | solution.py:27
Sparse Core Ops, SparseCore 0:
  13.1 131.6 all-gather.2
where the time goes:
time: 304 us; the launch traced here: 303 us
  blocking collectives  226 us (74%)
  starting transfers between devices  34 us (11%)
  local copies, waits for them, and re-layouts  14.8 us (5%)
  between operations  14.1 us (5%)
  other arithmetic  5.27 us (2%)
  waiting for transfers between devices  4.19 us (1%)
  matrix products  4.16 us (1%)
    all_gather x1, blocking collectives, side_by_side(): filled, at, outs = (lax.all_gather(both, axis, axis=dim, tiled=True), 0, [])  200 us
    all_to_all x1, starting transfers between devices, sent_and_summed(): lax.all_to_all(tiles, axis, split_axis=0, concat_axis=0, tiled=True)  34 us
    all_to_all x1, blocking collectives, sent_and_summed(): lax.all_to_all(tiles, axis, split_axis=0, concat_axis=0, tiled=True)  26.2 us
  transfers between devices with their start and end apart: 2, of which 1 were waited for; matrix products, arithmetic and copies ran while one was open for 2% of the time, Pallas kernels for 0%

commit v1 on v0

v1 whole, which is shorter than its diff:
```python
import math

import jax
import jax.numpy as jnp
from jax import lax
from jax.experimental import pallas as pl
from jax.experimental.pallas import tpu as pltpu
from jax.sharding import PartitionSpec as P

MESH = pl.DeviceIdType.MESH
DH = 128
NZ, NX, NY = 2, 4, 8
HEADS = 8
ROWS = 16
TOK = 384
COL = 256
BLK = NY * ROWS
SCALE = 1.0 / math.sqrt(DH)
LOG2E = math.log2(math.e)


def ring_offset(i, n):
    d = i // 2 + 1
    odd = i % 2
    return (1 - odd) * d + odd * (n - d)


def kernel(
    q_hbm, g_hbm, o_hbm, lse_hbm, k_hbm, v_hbm, cnt, w_hbm,
    kg_hbm, vg_hbm, qg_out, gg_out,
    qg, att, lse_v, kb, vb, kt, wb,
    ldb, ldg, dk, dv, dqs, dqo, rs1, redb, rs2, gs, gr, kob, vob,
    sem_in, sem_out, s_z, s_y, s_yl, s_x, s_xl, s_r1, s_r2, s_g,
    r_q, r_l, r_lg, r_r1, r_r2, r_g,
):
    obs = lax.axis_index("obs")
    head = lax.axis_index("head")
    z = obs // (NX * NY)
    x = (obs // NY) % NX
    y = obs % NY
    zo = 1 - z

    def dev(zz, xx, yy):
        return ((zz * NX + xx) * NY + yy, head)

    def slot(zz, xx, yy):
        return (zz * NX + xx) * NY + yy

    def xpeer(i):
        return (x + ring_offset(i, NX)) % NX

    def xsource(i):
        return (x + NX - ring_offset(i, NX)) % NX

    def ypeer(i):
        return (y + ring_offset(i, NY)) % NY

    def remote(src, dst, ssem, rsem, device):
        return pltpu.make_async_remote_copy(
            src_ref=src, dst_ref=dst, send_sem=ssem, recv_sem=rsem,
            device_id=device, device_id_type=MESH)

    me = slot(z, x, y)
    loads = [
        pltpu.make_async_copy(q_hbm, qg.at[me, :, pl.ds(0, COL)], sem_in.at[0]),
        pltpu.make_async_copy(g_hbm, qg.at[me, :, pl.ds(COL, COL)], sem_in.at[1]),
        pltpu.make_async_copy(o_hbm, att, sem_in.at[2]),
        pltpu.make_async_copy(lse_hbm, lse_v, sem_in.at[3]),
        pltpu.make_async_copy(k_hbm, kb, sem_in.at[4]),
        pltpu.make_async_copy(v_hbm, vb, sem_in.at[5]),
        pltpu.make_async_copy(w_hbm, wb, sem_in.at[6]),
    ]
    for c in loads:
        c.start()

    barrier = pltpu.get_barrier_semaphore()

    def hello(device):
        pl.semaphore_signal(barrier, inc=1, device_id=device, device_id_type=MESH)

    hello(dev(zo, x, y))

    def hello_y(i, c):
        hello(dev(z, x, ypeer(i)))
        hello(dev(zo, x, ypeer(i)))
        return c

    lax.fori_loop(0, NY - 1, hello_y, 0)

    def hello_x(i, c):
        hello(dev(z, xpeer(i), y))
        return c

    lax.fori_loop(0, NX - 1, hello_x, 0)

    def hello_h(i, c):
        hello((obs, (head + 1 + i) % HEADS))
        return c

    lax.fori_loop(0, HEADS - 1, hello_h, 0)

    for c in loads[:4]:
        c.wait()

    row = lax.broadcasted_iota(jnp.int32, (ROWS, BLK), 0)
    lane = lax.broadcasted_iota(jnp.int32, (ROWS, BLK), 1)
    mine = lane == row + y * ROWS
    own = z * NY + y
    for h in range(2):
        og = qg[me, :, COL + h * DH : COL + (h + 1) * DH].astype(jnp.float32)
        ao = att[:, h * DH : (h + 1) * DH].astype(jnp.float32)
        delta = jnp.sum(og * ao, axis=1, keepdims=True)
        lse = lse_v[:, h : h + 1] * LOG2E
        ldb[own, h : h + 1, :] = jnp.sum(jnp.where(mine, lse, 0.0), axis=0, keepdims=True)
        ldb[own, 2 + h : 3 + h, :] = jnp.sum(jnp.where(mine, delta, 0.0), axis=0, keepdims=True)

    pl.semaphore_wait(barrier, 1 + 2 * (NY - 1) + NX - 1 + HEADS - 1)

    def z_copy(k):
        if k == 0:
            return remote(qg.at[me], qg.at[me], s_z.at[0], r_q.at[me], dev(zo, x, y))
        return remote(ldb.at[own], ldb.at[own], s_z.at[1], r_l.at[own], dev(zo, x, y))

    def y_copies(zz, i):
        s = slot(zz, x, y)
        l = zz * NY + y
        n = zz * (NY - 1) + i
        to = dev(z, x, ypeer(i))
        return (remote(qg.at[s], qg.at[s], s_y.at[n], r_q.at[s], to),
                remote(ldb.at[l], ldb.at[l], s_yl.at[n], r_l.at[l], to))

    def x_copy(zz, yy, i):
        s = slot(zz, x, yy)
        n = (zz * NY + yy) * (NX - 1) + i
        return remote(qg.at[s], qg.at[s], s_x.at[n], r_q.at[s], dev(z, xpeer(i), y))

    def xl_copy(zz, i):
        n = zz * NX + x
        return remote(ldg.at[n], ldg.at[n], s_xl.at[zz * (NX - 1) + i], r_lg.at[n], dev(z, xpeer(i), y))

    def wait_q(s):
        remote(qg.at[s], qg.at[s], s_z.at[0], r_q.at[s], dev(zo, x, y)).wait_recv()

    def wait_l(l):
        remote(ldb.at[l], ldb.at[l], s_z.at[1], r_l.at[l], dev(zo, x, y)).wait_recv()

    def wait_lg(n):
        remote(ldg.at[n], ldg.at[n], s_z.at[1], r_lg.at[n], dev(zo, x, y)).wait_recv()

    def spread_y(zz):
        def body(i, c):
            for copy in y_copies(zz, i):
                copy.start()
            return c
        lax.fori_loop(0, NY - 1, body, 0)

    def spread_x(zz, yy):
        def body(i, c):
            x_copy(zz, yy, i).start()
            return c
        lax.fori_loop(0, NX - 1, body, 0)

    def pass_on(zz):
        def body(i, c):
            yy = ypeer(i)
            wait_q(slot(zz, x, yy))
            spread_x(zz, yy)
            return c
        lax.fori_loop(0, NY - 1, body, 0)

        def body_l(i, c):
            wait_l(zz * NY + ypeer(i))
            return c
        lax.fori_loop(0, NY - 1, body_l, 0)
        total = ldb[zz * NY]
        for k in range(1, NY):
            total = total + ldb[zz * NY + k]
        ldg[zz * NX + x] = total

        def body_g(i, c):
            xl_copy(zz, i).start()
            return c
        lax.fori_loop(0, NX - 1, body_g, 0)

    z_copy(0).start()
    z_copy(1).start()
    spread_y(z)
    spread_x(z, y)

    for c in loads[4:]:
        c.wait()
    for h in range(2):
        kt[h] = kb[:, h * DH : (h + 1) * DH].astype(jnp.float32).T.astype(jnp.bfloat16)
    dk[...] = jnp.zeros_like(dk)
    dv[...] = jnp.zeros_like(dv)
    live = lax.broadcasted_iota(jnp.int32, (TOK, BLK), 0) < cnt[0]

    def adjoint(zz, xx):
        base = slot(zz, xx, 0)
        parts = []
        for h in range(2):
            cols = slice(h * DH, (h + 1) * DH)
            qh = qg[pl.ds(base, NY), :, h * DH : (h + 1) * DH].reshape(BLK, DH)
            gh = qg[pl.ds(base, NY), :, COL + h * DH : COL + (h + 1) * DH].reshape(BLK, DH)
            lse = ldg[zz * NX + xx, h : h + 1, :]
            delta = ldg[zz * NX + xx, 2 + h : 3 + h, :]
            nt = (((1,), (1,)), ((), ()))
            scores = lax.dot_general(kb[:, cols], qh, nt, preferred_element_type=jnp.float32)
            dprobs = lax.dot_general(vb[:, cols], gh, nt, preferred_element_type=jnp.float32)
            probs = jnp.where(live, jnp.exp2(scores * (SCALE * LOG2E) - lse), 0.0)
            dscores = (probs * (dprobs - delta)).astype(jnp.bfloat16)
            dv[:, cols] += jnp.dot(probs.astype(jnp.bfloat16), gh, preferred_element_type=jnp.float32)
            dk[:, cols] += jnp.dot(dscores, qh, preferred_element_type=jnp.float32)
            dqt = jnp.dot(kt[h], dscores, preferred_element_type=jnp.float32)
            parts.append(dqt.T)
        return parts

    def own_group(zz):
        parts = adjoint(zz, x)
        for h in range(2):
            dqo[zz, :, h * DH : (h + 1) * DH] = parts[h]

    def r1_copy(zz, i):
        n = zz * (NX - 1) + i
        return remote(dqs.at[n], rs1.at[n], s_r1.at[n], r_r1.at[n], dev(z, xpeer(i), y))

    def other_groups(zz):
        def body(i, c):
            xx = xpeer(i)

            def arrive(yy, c2):
                wait_q(slot(zz, xx, yy))
                return c2
            lax.fori_loop(0, NY, arrive, 0)
            wait_lg(zz * NX + xx)
            parts = adjoint(zz, xx)
            n = zz * (NX - 1) + i
            for h in range(2):
                dqs[n, :, :, h * DH : (h + 1) * DH] = parts[h].astype(jnp.bfloat16).reshape(NY, ROWS, DH)
            r1_copy(zz, i).start()
            return c
        lax.fori_loop(0, NX - 1, body, 0)

    def r2_copy(zz, yy):
        n = zz * NY + yy
        return remote(redb.at[n], rs2.at[own], s_r2.at[n], r_r2.at[own], dev(zz, x, yy))

    def reduce_x(zz):
        for i in range(NX - 1):
            r1_copy(zz, i).wait_recv()
        total = dqo[zz]
        for i in range(NX - 1):
            total = total + rs1[zz * (NX - 1) + i].reshape(BLK, COL).astype(jnp.float32)
        redb[pl.ds(zz * NY, NY)] = total.astype(jnp.bfloat16).reshape(NY, ROWS, COL)

    pass_on(z)
    own_group(z)
    wait_q(slot(zo, x, y))
    wait_l(zo * NY + y)
    spread_y(zo)
    spread_x(zo, y)
    other_groups(z)
    pass_on(zo)
    own_group(zo)
    reduce_x(z)

    def near(i, c):
        r2_copy(z, ypeer(i)).start()
        return c
    lax.fori_loop(0, NY - 1, near, 0)
    rs2[own] = redb[own]
    other_groups(zo)
    kob[...] = (dk[...] * SCALE).astype(jnp.bfloat16)
    vob[...] = dv[...].astype(jnp.bfloat16)
    outs = [pltpu.make_async_copy(kob, kg_hbm, sem_out.at[0]),
            pltpu.make_async_copy(vob, vg_hbm, sem_out.at[1])]
    for c in outs:
        c.start()
    reduce_x(zo)

    def far(i, c):
        r2_copy(zo, (y + i) % NY).start()
        return c
    lax.fori_loop(0, NY, far, 0)

    def landed_near(i, c):
        l = z * NY + ypeer(i)
        remote(rs2.at[l], rs2.at[l], s_z.at[0], r_r2.at[l], dev(zo, x, y)).wait_recv()
        return c
    lax.fori_loop(0, NY - 1, landed_near, 0)

    def landed_far(i, c):
        l = zo * NY + i
        remote(rs2.at[l], rs2.at[l], s_z.at[0], r_r2.at[l], dev(zo, x, y)).wait_recv()
        return c
    lax.fori_loop(0, NY, landed_far, 0)

    query_half = (jnp.sum(rs2[...].astype(jnp.float32), axis=0) * SCALE).astype(jnp.bfloat16)
    qg_out[...] = query_half

    def g_copy(j):
        return remote(gs.at[j], gr.at[head], s_g.at[j], r_g.at[head], (obs, j))

    def grid_block(i, c):
        j = (head + 1 + i) % HEADS
        part = lax.dot_general(query_half, wb[pl.ds(j * COL, COL), :], (((1,), (1,)), ((), ())),
                               preferred_element_type=jnp.float32)
        gs[j] = part
        g_copy(j).start()
        return c
    lax.fori_loop(0, HEADS - 1, grid_block, 0)
    gr[head] = lax.dot_general(query_half, wb[pl.ds(head * COL, COL), :], (((1,), (1,)), ((), ())),
                               preferred_element_type=jnp.float32)

    def grid_landed(i, c):
        j = (head + 1 + i) % HEADS
        remote(gr.at[j], gr.at[j], s_g.at[j], r_g.at[j], (obs, j)).wait_recv()
        return c
    lax.fori_loop(0, HEADS - 1, grid_landed, 0)
    gg_out[...] = jnp.sum(gr[...], axis=0).astype(jnp.bfloat16)

    z_copy(0).wait_send()
    z_copy(1).wait_send()

    def sent_y(i, c):
        for zz in (z, zo):
            for copy in y_copies(zz, i):
                copy.wait_send()
        return c
    lax.fori_loop(0, NY - 1, sent_y, 0)

    def sent_x(i, c):
        def inner(yy, c2):
            x_copy(0, yy, i).wait_send()
            x_copy(1, yy, i).wait_send()
            return c2
        lax.fori_loop(0, NY, inner, 0)
        for zz in range(NZ):
            xl_copy(zz, i).wait_send()
            r1_copy(zz, i).wait_send()
        return c
    lax.fori_loop(0, NX - 1, sent_x, 0)

    def sent_near(i, c):
        r2_copy(z, ypeer(i)).wait_send()
        return c
    lax.fori_loop(0, NY - 1, sent_near, 0)

    def sent_far(i, c):
        r2_copy(zo, i).wait_send()
        return c
    lax.fori_loop(0, NY, sent_far, 0)

    def sent_g(i, c):
        g_copy((head + 1 + i) % HEADS).wait_send()
        return c
    lax.fori_loop(0, HEADS - 1, sent_g, 0)
    for c in outs:
        c.wait()


def on_device(queries, out_grad, attn_out, logsumexp, keys, values, obs_counts, query_weight):
    bf, f32 = jnp.bfloat16, jnp.float32
    anywhere = pl.BlockSpec(memory_space=pl.ANY)
    vmem = pl.BlockSpec(memory_space=pltpu.VMEM)
    dma = pltpu.SemaphoreType.DMA
    blocks = NZ * NX * NY
    return pl.pallas_call(
        kernel,
        name="adjoint",
        out_shape=(
            jax.ShapeDtypeStruct((TOK, COL), bf),
            jax.ShapeDtypeStruct((TOK, COL), bf),
            jax.ShapeDtypeStruct((ROWS, COL), bf),
            jax.ShapeDtypeStruct((ROWS, COL), bf),
        ),
        in_specs=[anywhere] * 6 + [pl.BlockSpec(memory_space=pltpu.SMEM), anywhere],
        out_specs=(anywhere, anywhere, vmem, vmem),
        scratch_shapes=[
            pltpu.VMEM((blocks, ROWS, 2 * COL), bf),
            pltpu.VMEM((ROWS, COL), bf),
            pltpu.VMEM((ROWS, 2), f32),
            pltpu.VMEM((TOK, COL), bf),
            pltpu.VMEM((TOK, COL), bf),
            pltpu.VMEM((2, DH, TOK), bf),
            pltpu.VMEM((HEADS * COL, COL), bf),
            pltpu.VMEM((NZ * NY, 4, BLK), f32),
            pltpu.VMEM((NZ * NX, 4, BLK), f32),
            pltpu.VMEM((TOK, COL), f32),
            pltpu.VMEM((TOK, COL), f32),
            pltpu.VMEM((NZ * (NX - 1), NY, ROWS, COL), bf),
            pltpu.VMEM((NZ, BLK, COL), f32),
            pltpu.VMEM((NZ * (NX - 1), NY, ROWS, COL), bf),
            pltpu.VMEM((NZ * NY, ROWS, COL), bf),
            pltpu.VMEM((NZ * NY, ROWS, COL), bf),
            pltpu.VMEM((HEADS, ROWS, COL), f32),
            pltpu.VMEM((HEADS, ROWS, COL), f32),
            pltpu.VMEM((TOK, COL), bf),
            pltpu.VMEM((TOK, COL), bf),
            dma((7,)), dma((2,)), dma((2,)), dma((NZ * (NY - 1),)), dma((NZ * (NY - 1),)),
            dma((NZ * NY * (NX - 1),)), dma((NZ * (NX - 1),)), dma((NZ * (NX - 1),)),
            dma((NZ * NY,)), dma((HEADS,)),
            dma((blocks,)), dma((NZ * NY,)), dma((NZ * NX,)), dma((NZ * (NX - 1),)),
            dma((NZ * NY,)), dma((HEADS,)),
        ],
        compiler_params=pltpu.CompilerParams(collective_id=0, has_side_effects=True),
    )(queries, out_grad, attn_out, logsumexp, keys, values, obs_counts, query_weight)


def solution(mesh):
    in_specs = (
        P("obs", "head"),
        P("obs", "head"),
        P("obs", "head"),
        P("obs", "head"),
        P("obs", "head"),
        P("obs", "head"),
        P("obs"),
        P(None, "head"),
    )
    out_specs = (P("obs", "head"), P("obs", "head"), P("obs", "head"), P("obs", "head"))
    return jax.shard_map(
        on_device, mesh=mesh, in_specs=in_specs, out_specs=out_specs, check_vma=False
    )
```

time: 304 us -> 62.4 us (0.21)
  blocking collectives: 226 us -> 0 us
  Pallas kernels: 0 us -> 56.5 us
  starting transfers between devices: 34 us -> 0 us
  between operations: 14.1 us -> 1.32 us
  local copies, waits for them, and re-layouts: 14.8 us -> 4.35 us
  other arithmetic: 5.27 us -> 0 us
  waiting for transfers between devices: 4.19 us -> 0 us
  matrix products: 4.16 us -> 0 us
    all_gather x1 -> x0, blocking collectives: 200 us -> none  [side_by_side(): filled, at, outs = (lax.all_gather(both, axis, axis=dim, tiled=True), 0, [])]
    pallas_call x0 -> x1, Pallas kernels: none -> 56.5 us  [on_device(): pl.pallas_call(kernel, name='adjoint', out_shape=(jax.ShapeDtypeStruct((T...]
    all_to_all x1 -> x0, starting transfers between devices: 34 us -> none  [sent_and_summed(): lax.all_to_all(tiles, axis, split_axis=0, concat_axis=0, tiled=True)]
    all_to_all x1 -> x0, blocking collectives: 26.2 us -> none  [sent_and_summed(): lax.all_to_all(tiles, axis, split_axis=0, concat_axis=0, tiled=True)]
    dynamic_slice x8 -> x0, local copies, waits for them, and re-layouts: 4.46 us -> none  [the longest x4 2.23 us: visit_rows(): query_rows = lax.dynamic_slice_in_dim(query_part, offset, block_rows, 0)]
    dot_general x11 -> x0, matrix products: 4.16 us -> none  [the longest x2 0.96 us: adjoint(): jnp.einsum('qhd,khd->hqk', query_heads, key_heads, preferred_element_type...]
    all_to_all x1 -> x0, waiting for transfers between devices: 4.15 us -> none  [sent_and_summed(): lax.all_to_all(tiles, axis, split_axis=0, concat_axis=0, tiled=True)]
  transfers between devices with their start and end apart: 2 -> 0, of which waited for: 1 -> 0; matrix products, arithmetic and copies ran while one was open for 2% -> 0% of each run, Pallas kernels for 0% -> 0%
where the time goes in v1:
time: 62.4 us; the launch traced here: 62.1 us
  Pallas kernels  56.5 us (91%)
  local copies, waits for them, and re-layouts  4.35 us (7%)
  between operations  1.32 us (2%)
    pallas_call x1, Pallas kernels, on_device(): pl.pallas_call(kernel, name='adjoint', out_shape=(jax.ShapeDtypeStruct((T...  56.5 us
    unnamed x13, local copies, waits for them, and re-layouts  4.35 us

profile of v1, /device:TPU:1, one launch (start us, length us, event | category | flops | bytes accessed | tf_op | source)
XLA Modules:
  0.0 62.1 jit_solution(176652868954325661)
XLA Ops:
  0.6 0.0 copy-start.3
  1.3 0.0 copy-done.3
  1.3 0.7 %copy.12.lse_hbm = f32[16,2]{1,0:T(8,128)} copy(f32[16,2]{0,1:T(2,128)S(1)} %copy-done.3) | data formatting | bytes 256 | tf_op args[3]
  2.0 56.5 %adjoint.1 = (bf16[384,256]{1,0:T(8,128)(2,1)}, bf16[384,256]{1,0:T(8,128)(2,1)}, bf16[16,256]{1,0:T(8,128)(2,1)}, bf16[16,256]{1,0:T(8,128)(2,1)}) custom-call(bf16[16,256]{1,0:T(8,128)(2,1)} %q_hbm.1, bf16[16,256]{1,0:T(8,128)(2,1)} %g_hbm.1, bf16[16,256]{1,0:T(8,128)(2,1)} %o_hbm.1, f32[16,2]{1,0:T(8,128)} %copy.12.lse_hbm, bf16[384,256]{1,0:T(8,128)(2,1)} %k_hbm.1, ...), custom_call_target="tpu_custom_call" | custom-call | tf_op jit(solution)/shard_map/adjoint/pallas_call | solution.py:368
  58.5 0.0 copy-start
  58.5 1.7 %copy.18 = bf16[384,256]{1,0:T(8,128)(2,1)} copy(bf16[384,256]{1,0:T(8,128)(2,1)} %get-tuple-element.8) | data formatting | bytes 393216
  60.1 0.0 copy-done
  60.1 0.0 copy-start.2
  60.1 0.7 %copy.19 = bf16[384,256]{1,0:T(8,128)(2,1)} copy(bf16[384,256]{1,0:T(8,128)(2,1)S(1)} %copy-done) | data formatting | bytes 393216
  60.8 0.0 copy-done.2
  60.8 0.0 copy-start.1
  60.8 0.6 copy.20
  61.4 0.1 copy-done.1
  61.5 0.6 copy.21
Async XLA Ops:
  0.6 0.7 %copy-start.3 = (f32[16,2]{0,1:T(2,128)S(1)}, f32[16,2]{0,1:T(2,128)}, u32[]{:S(2)}) copy-start(f32[16,2]{0,1:T(2,128)} %param.11) | copy-start | bytes 388
  58.5 1.7 %copy-start = (bf16[384,256]{1,0:T(8,128)(2,1)S(1)}, bf16[384,256]{1,0:T(8,128)(2,1)}, u32[]{:S(2)}) copy-start(bf16[384,256]{1,0:T(8,128)(2,1)} %get-tuple-element.9) | copy-start | bytes 589828
  60.1 0.7 %copy-start.2 = (bf16[16,256]{1,0:T(8,128)(2,1)S(1)}, bf16[16,256]{1,0:T(8,128)(2,1)}, u32[]{:S(2)}) copy-start(bf16[16,256]{1,0:T(8,128)(2,1)} %get-tuple-element.10) | copy-start | bytes 24580
  60.8 0.7 %copy-start.1 = (bf16[16,256]{1,0:T(8,128)(2,1)S(1)}, bf16[16,256]{1,0:T(8,128)(2,1)}, u32[]{:S(2)}) copy-start(bf16[16,256]{1,0:T(8,128)(2,1)} %get-tuple-element.11) | copy-start | bytes 24580

commit v2 on v1

--- a/solution.py
+++ b/solution.py
@@ -27,10 +27,10 @@
 
 def kernel(
     q_hbm, g_hbm, o_hbm, lse_hbm, k_hbm, v_hbm, cnt, w_hbm,
-    kg_hbm, vg_hbm, qg_out, gg_out,
+    kob, vob, qg_out, gg_out,
     qg, att, lse_v, kb, vb, kt, wb,
-    ldb, ldg, dk, dv, dqs, dqo, rs1, redb, rs2, gs, gr, kob, vob,
-    sem_in, sem_out, s_z, s_y, s_yl, s_x, s_xl, s_r1, s_r2, s_g,
+    ldb, ldg, dk, dv, dqs, dqo, rs1, redb, rs2, gs, gr,
+    sem_in, s_z, s_y, s_yl, s_x, s_xl, s_r1, s_r2, s_g,
     r_q, r_l, r_lg, r_r1, r_r2, r_g,
 ):
     obs = lax.axis_index("obs")
@@ -82,7 +82,6 @@
 
     def hello_y(i, c):
         hello(dev(z, x, ypeer(i)))
-        hello(dev(zo, x, ypeer(i)))
         return c
 
     lax.fori_loop(0, NY - 1, hello_y, 0)
@@ -105,16 +104,17 @@
     row = lax.broadcasted_iota(jnp.int32, (ROWS, BLK), 0)
     lane = lax.broadcasted_iota(jnp.int32, (ROWS, BLK), 1)
     mine = lane == row + y * ROWS
+    my_lanes = lax.broadcasted_iota(jnp.int32, (1, BLK), 1) // ROWS == y
     own = z * NY + y
     for h in range(2):
         og = qg[me, :, COL + h * DH : COL + (h + 1) * DH].astype(jnp.float32)
         ao = att[:, h * DH : (h + 1) * DH].astype(jnp.float32)
         delta = jnp.sum(og * ao, axis=1, keepdims=True)
-        lse = lse_v[:, h : h + 1] * LOG2E
-        ldb[own, h : h + 1, :] = jnp.sum(jnp.where(mine, lse, 0.0), axis=0, keepdims=True)
+        lse = jnp.concatenate([lse_v[h : h + 1, :] * LOG2E] * NY, axis=1)
+        ldb[own, h : h + 1, :] = jnp.where(my_lanes, lse, 0.0)
         ldb[own, 2 + h : 3 + h, :] = jnp.sum(jnp.where(mine, delta, 0.0), axis=0, keepdims=True)
 
-    pl.semaphore_wait(barrier, 1 + 2 * (NY - 1) + NX - 1 + HEADS - 1)
+    pl.semaphore_wait(barrier, 1 + NY - 1 + NX - 1 + HEADS - 1)
 
     def z_copy(k):
         if k == 0:
@@ -224,13 +224,14 @@
         n = zz * (NX - 1) + i
         return remote(dqs.at[n], rs1.at[n], s_r1.at[n], r_r1.at[n], dev(z, xpeer(i), y))
 
-    def other_groups(zz):
+    def other_groups(zz, first, last):
         def body(i, c):
             xx = xpeer(i)
 
-            def arrive(yy, c2):
-                wait_q(slot(zz, xx, yy))
+            def arrive(k, c2):
+                wait_q(slot(zz, xx, k))
                 return c2
+
             lax.fori_loop(0, NY, arrive, 0)
             wait_lg(zz * NX + xx)
             parts = adjoint(zz, xx)
@@ -239,7 +240,7 @@
                 dqs[n, :, :, h * DH : (h + 1) * DH] = parts[h].astype(jnp.bfloat16).reshape(NY, ROWS, DH)
             r1_copy(zz, i).start()
             return c
-        lax.fori_loop(0, NX - 1, body, 0)
+        lax.fori_loop(first, last, body, 0)
 
     def r2_copy(zz, yy):
         n = zz * NY + yy
@@ -254,14 +255,17 @@
         redb[pl.ds(zz * NY, NY)] = total.astype(jnp.bfloat16).reshape(NY, ROWS, COL)
 
     pass_on(z)
-    own_group(z)
     wait_q(slot(zo, x, y))
     wait_l(zo * NY + y)
     spread_y(zo)
     spread_x(zo, y)
-    other_groups(z)
     pass_on(zo)
+    own_group(z)
     own_group(zo)
+    other_groups(z, 0, 2)
+    other_groups(zo, 0, 2)
+    other_groups(z, 2, 3)
+    other_groups(zo, 2, 3)
     reduce_x(z)
 
     def near(i, c):
@@ -269,13 +273,8 @@
         return c
     lax.fori_loop(0, NY - 1, near, 0)
     rs2[own] = redb[own]
-    other_groups(zo)
     kob[...] = (dk[...] * SCALE).astype(jnp.bfloat16)
     vob[...] = dv[...].astype(jnp.bfloat16)
-    outs = [pltpu.make_async_copy(kob, kg_hbm, sem_out.at[0]),
-            pltpu.make_async_copy(vob, vg_hbm, sem_out.at[1])]
-    for c in outs:
-        c.start()
     reduce_x(zo)
 
     def far(i, c):
@@ -301,16 +300,15 @@
     def g_copy(j):
         return remote(gs.at[j], gr.at[head], s_g.at[j], r_g.at[head], (obs, j))
 
-    def grid_block(i, c):
-        j = (head + 1 + i) % HEADS
-        part = lax.dot_general(query_half, wb[pl.ds(j * COL, COL), :], (((1,), (1,)), ((), ())),
-                               preferred_element_type=jnp.float32)
-        gs[j] = part
-        g_copy(j).start()
-        return c
-    lax.fori_loop(0, HEADS - 1, grid_block, 0)
-    gr[head] = lax.dot_general(query_half, wb[pl.ds(head * COL, COL), :], (((1,), (1,)), ((), ())),
-                               preferred_element_type=jnp.float32)
+    parts = lax.dot_general(query_half, wb[...], (((1,), (1,)), ((), ())), preferred_element_type=jnp.float32)
+    for j in range(HEADS):
+        gs[j] = parts[:, j * COL : (j + 1) * COL]
+
+    def grid_send(i, c):
+        g_copy((head + 1 + i) % HEADS).start()
+        return c
+    lax.fori_loop(0, HEADS - 1, grid_send, 0)
+    gr[head] = gs[head]
 
     def grid_landed(i, c):
         j = (head + 1 + i) % HEADS
@@ -355,7 +353,14 @@
         g_copy((head + 1 + i) % HEADS).wait_send()
         return c
     lax.fori_loop(0, HEADS - 1, sent_g, 0)
-    for c in outs:
+
+
+def finish(kob, vob, qgo, ggo, kg_hbm, vg_hbm, qg_hbm, gg_hbm, sem):
+    pairs = ((qgo, qg_hbm), (ggo, gg_hbm), (kob, kg_hbm), (vob, vg_hbm))
+    copies = [pltpu.make_async_copy(a, b, sem.at[i]) for i, (a, b) in enumerate(pairs)]
+    for c in copies:
+        c.start()
+    for c in copies:
         c.wait()
 
 
@@ -365,21 +370,17 @@
     vmem = pl.BlockSpec(memory_space=pltpu.VMEM)
     dma = pltpu.SemaphoreType.DMA
     blocks = NZ * NX * NY
-    return pl.pallas_call(
+    shapes = ((TOK, COL), (TOK, COL), (ROWS, COL), (ROWS, COL))
+    held = pl.pallas_call(
         kernel,
         name="adjoint",
-        out_shape=(
-            jax.ShapeDtypeStruct((TOK, COL), bf),
-            jax.ShapeDtypeStruct((TOK, COL), bf),
-            jax.ShapeDtypeStruct((ROWS, COL), bf),
-            jax.ShapeDtypeStruct((ROWS, COL), bf),
-        ),
+        out_shape=tuple(pltpu.VMEM(shape, bf) for shape in shapes),
         in_specs=[anywhere] * 6 + [pl.BlockSpec(memory_space=pltpu.SMEM), anywhere],
-        out_specs=(anywhere, anywhere, vmem, vmem),
+        out_specs=(vmem,) * 4,
         scratch_shapes=[
             pltpu.VMEM((blocks, ROWS, 2 * COL), bf),
             pltpu.VMEM((ROWS, COL), bf),
-            pltpu.VMEM((ROWS, 2), f32),
+            pltpu.VMEM((2, ROWS), f32),
             pltpu.VMEM((TOK, COL), bf),
             pltpu.VMEM((TOK, COL), bf),
             pltpu.VMEM((2, DH, TOK), bf),
@@ -395,16 +396,22 @@
             pltpu.VMEM((NZ * NY, ROWS, COL), bf),
             pltpu.VMEM((HEADS, ROWS, COL), f32),
             pltpu.VMEM((HEADS, ROWS, COL), f32),
-            pltpu.VMEM((TOK, COL), bf),
-            pltpu.VMEM((TOK, COL), bf),
-            dma((7,)), dma((2,)), dma((2,)), dma((NZ * (NY - 1),)), dma((NZ * (NY - 1),)),
+            dma((7,)), dma((2,)), dma((NZ * (NY - 1),)), dma((NZ * (NY - 1),)),
             dma((NZ * NY * (NX - 1),)), dma((NZ * (NX - 1),)), dma((NZ * (NX - 1),)),
             dma((NZ * NY,)), dma((HEADS,)),
             dma((blocks,)), dma((NZ * NY,)), dma((NZ * NX,)), dma((NZ * (NX - 1),)),
             dma((NZ * NY,)), dma((HEADS,)),
         ],
         compiler_params=pltpu.CompilerParams(collective_id=0, has_side_effects=True),
-    )(queries, out_grad, attn_out, logsumexp, keys, values, obs_counts, query_weight)
+    )(queries, out_grad, attn_out, logsumexp.T, keys, values, obs_counts, query_weight)
+    return pl.pallas_call(
+        finish,
+        name="finish",
+        out_shape=tuple(jax.ShapeDtypeStruct(shape, bf) for shape in shapes),
+        in_specs=[vmem] * 4,
+        out_specs=(anywhere,) * 4,
+        scratch_shapes=[dma((4,))],
+    )(*[pltpu.with_memory_space_constraint(a, pltpu.VMEM) for a in held])
 
 
 def solution(mesh):

time: 62.4 us -> 55.6 us (0.89)
  local copies, waits for them, and re-layouts: 4.35 us -> 0 us
  Pallas kernels: 56.5 us -> 54.2 us
    unnamed x13 -> x0, local copies, waits for them, and re-layouts: 4.35 us -> none
    pallas_call x1 -> x2, Pallas kernels: 56.5 us -> 54.2 us  [the longest x1 53.4 us: on_device(): pl.pallas_call(kernel, name='adjoint', out_shape=tuple((pltpu.VMEM(shape,...]
where the time goes in v2:
time: 55.6 us; the launch traced here: 55.5 us
  Pallas kernels  54.2 us (97%)
  between operations  1.29 us (2%)
    pallas_call x1, Pallas kernels, on_device(): pl.pallas_call(kernel, name='adjoint', out_shape=tuple((pltpu.VMEM(shape,...  53.4 us

profile of v2, /device:TPU:1, one launch (start us, length us, event | category | flops | bytes accessed | tf_op | source)
XLA Modules:
  0.0 55.5 jit_solution(14113443898152704923)
XLA Ops:
  1.3 53.4 %adjoint.1 = (bf16[384,256]{1,0:T(8,128)(2,1)S(1)}, bf16[384,256]{1,0:T(8,128)(2,1)S(1)}, bf16[16,256]{1,0:T(8,128)(2,1)S(1)}, bf16[16,256]{1,0:T(8,128)(2,1)S(1)}) custom-call(bf16[16,256]{1,0:T(8,128)(2,1)} %q_hbm.1, bf16[16,256]{1,0:T(8,128)(2,1)} %g_hbm.1, bf16[16,256]{1,0:T(8,128)(2,1)} %o_hbm.1, f32[2,16]{1,0:T(2,128)} %bitcast.1, ...), custom_call_target="tpu_custom_call" | custom-call | tf_op jit(solution)/shard_map/adjoint/pallas_call | solution.py:374
  54.7 0.8 %finish.1 = (bf16[384,256]{1,0:T(8,128)(2,1)}, bf16[384,256]{1,0:T(8,128)(2,1)}, bf16[16,256]{1,0:T(8,128)(2,1)}, bf16[16,256]{1,0:T(8,128)(2,1)}) custom-call(bf16[384,256]{1,0:T(8,128)(2,1)S(1)} %get-tuple-element.8.kob, bf16[384,256]{1,0:T(8,128)(2,1)S(1)} %get-tuple-element.9.vob, bf16[16,256]{1,0:T(8,128)(2,1)S(1)} %get-tuple-element.10.qgo, ...), custom_call_target="tpu_custom_call" | custom-call | tf_op jit(solution)/shard_map/finish/pallas_call | solution.py:407

commit v3 on v2

--- a/solution.py
+++ b/solution.py
@@ -31,7 +31,7 @@
     qg, att, lse_v, kb, vb, kt, wb,
     ldb, ldg, dk, dv, dqs, dqo, rs1, redb, rs2, gs, gr,
     sem_in, s_z, s_y, s_yl, s_x, s_xl, s_r1, s_r2, s_g,
-    r_q, r_l, r_lg, r_r1, r_r2, r_g,
+    r_q, r_x, r_l, r_lg, r_r1, r_r2, r_g,
 ):
     obs = lax.axis_index("obs")
     head = lax.axis_index("head")
@@ -98,14 +98,99 @@
 
     lax.fori_loop(0, HEADS - 1, hello_h, 0)
 
-    for c in loads[:4]:
+    for c in loads[:2]:
+        c.wait()
+    own = z * NY + y
+    pl.semaphore_wait(barrier, 1 + NY - 1 + NX - 1 + HEADS - 1)
+
+    def z_copy(k):
+        if k == 0:
+            return remote(qg.at[me], qg.at[me], s_z.at[0], r_q.at[z * NY + y], dev(zo, x, y))
+        return remote(ldb.at[own], ldb.at[own], s_z.at[1], r_l.at[own], dev(zo, x, y))
+
+    def y_copies(zz, i):
+        s = slot(zz, x, y)
+        l = zz * NY + y
+        to = dev(z, x, ypeer(i))
+        return (remote(qg.at[s], qg.at[s], s_y.at[zz], r_q.at[l], to),
+                remote(ldb.at[l], ldb.at[l], s_yl.at[zz], r_l.at[l], to))
+
+    def strip(zz, xx):
+        return qg.at[pl.ds(slot(zz, xx, 0), NY)]
+
+    def row_copy(zz, i):
+        return remote(strip(zz, x), strip(zz, x), s_x.at[zz * (NX - 1) + i], r_x.at[zz * NX + x], dev(z, xpeer(i), y))
+
+    def x_copy(zz, yy, i):
+        s = slot(zz, x, yy)
+        return remote(qg.at[s], qg.at[s], s_x.at[zz * (NX - 1) + i], r_x.at[zz * NX + x], dev(z, xpeer(i), y))
+
+    def xl_copy(zz, i):
+        n = zz * NX + x
+        return remote(ldg.at[n], ldg.at[n], s_xl.at[zz * (NX - 1) + i], r_lg.at[n], dev(z, xpeer(i), y))
+
+    def wait_q(zz, yy):
+        s = slot(zz, x, yy)
+        remote(qg.at[s], qg.at[s], s_z.at[0], r_q.at[zz * NY + yy], dev(zo, x, y)).wait_recv()
+
+    def wait_row(zz, xx):
+        remote(strip(zz, xx), strip(zz, xx), s_x.at[0], r_x.at[zz * NX + xx], dev(z, xx, y)).wait_recv()
+
+    def wait_l(l):
+        remote(ldb.at[l], ldb.at[l], s_z.at[1], r_l.at[l], dev(zo, x, y)).wait_recv()
+
+    def wait_lg(n):
+        remote(ldg.at[n], ldg.at[n], s_z.at[1], r_lg.at[n], dev(zo, x, y)).wait_recv()
+
+    def spread_y(zz, which):
+        def body(i, c):
+            y_copies(zz, i)[which].start()
+            return c
+        lax.fori_loop(0, NY - 1, body, 0)
+
+    def spread_x(zz, yy):
+        def body(i, c):
+            x_copy(zz, yy, i).start()
+            return c
+        lax.fori_loop(0, NX - 1, body, 0)
+
+    def rows_in(zz, pieces):
+        def body(i, c):
+            yy = ypeer(i)
+            wait_q(zz, yy)
+            if pieces:
+                spread_x(zz, yy)
+            return c
+        lax.fori_loop(0, NY - 1, body, 0)
+        if not pieces:
+            for i in range(NX - 1):
+                row_copy(zz, i).start()
+
+        def body_l(i, c):
+            wait_l(zz * NY + ypeer(i))
+            return c
+        lax.fori_loop(0, NY - 1, body_l, 0)
+        total = ldb[zz * NY]
+        for k in range(1, NY):
+            total = total + ldb[zz * NY + k]
+        ldg[zz * NX + x] = total
+
+        def body_g(i, c):
+            xl_copy(zz, i).start()
+            return c
+        lax.fori_loop(0, NX - 1, body_g, 0)
+
+    z_copy(0).start()
+    spread_y(z, 0)
+    spread_x(z, y)
+
+    for c in loads[2:4]:
         c.wait()
 
     row = lax.broadcasted_iota(jnp.int32, (ROWS, BLK), 0)
     lane = lax.broadcasted_iota(jnp.int32, (ROWS, BLK), 1)
     mine = lane == row + y * ROWS
     my_lanes = lax.broadcasted_iota(jnp.int32, (1, BLK), 1) // ROWS == y
-    own = z * NY + y
     for h in range(2):
         og = qg[me, :, COL + h * DH : COL + (h + 1) * DH].astype(jnp.float32)
         ao = att[:, h * DH : (h + 1) * DH].astype(jnp.float32)
@@ -114,78 +199,8 @@
         ldb[own, h : h + 1, :] = jnp.where(my_lanes, lse, 0.0)
         ldb[own, 2 + h : 3 + h, :] = jnp.sum(jnp.where(mine, delta, 0.0), axis=0, keepdims=True)
 
-    pl.semaphore_wait(barrier, 1 + NY - 1 + NX - 1 + HEADS - 1)
-
-    def z_copy(k):
-        if k == 0:
-            return remote(qg.at[me], qg.at[me], s_z.at[0], r_q.at[me], dev(zo, x, y))
-        return remote(ldb.at[own], ldb.at[own], s_z.at[1], r_l.at[own], dev(zo, x, y))
-
-    def y_copies(zz, i):
-        s = slot(zz, x, y)
-        l = zz * NY + y
-        n = zz * (NY - 1) + i
-        to = dev(z, x, ypeer(i))
-        return (remote(qg.at[s], qg.at[s], s_y.at[n], r_q.at[s], to),
-                remote(ldb.at[l], ldb.at[l], s_yl.at[n], r_l.at[l], to))
-
-    def x_copy(zz, yy, i):
-        s = slot(zz, x, yy)
-        n = (zz * NY + yy) * (NX - 1) + i
-        return remote(qg.at[s], qg.at[s], s_x.at[n], r_q.at[s], dev(z, xpeer(i), y))
-
-    def xl_copy(zz, i):
-        n = zz * NX + x
-        return remote(ldg.at[n], ldg.at[n], s_xl.at[zz * (NX - 1) + i], r_lg.at[n], dev(z, xpeer(i), y))
-
-    def wait_q(s):
-        remote(qg.at[s], qg.at[s], s_z.at[0], r_q.at[s], dev(zo, x, y)).wait_recv()
-
-    def wait_l(l):
-        remote(ldb.at[l], ldb.at[l], s_z.at[1], r_l.at[l], dev(zo, x, y)).wait_recv()
-
-    def wait_lg(n):
-        remote(ldg.at[n], ldg.at[n], s_z.at[1], r_lg.at[n], dev(zo, x, y)).wait_recv()
-
-    def spread_y(zz):
-        def body(i, c):
-            for copy in y_copies(zz, i):
-                copy.start()
-            return c
-        lax.fori_loop(0, NY - 1, body, 0)
-
-    def spread_x(zz, yy):
-        def body(i, c):
-            x_copy(zz, yy, i).start()
-            return c
-        lax.fori_loop(0, NX - 1, body, 0)
-
-    def pass_on(zz):
-        def body(i, c):
-            yy = ypeer(i)
-            wait_q(slot(zz, x, yy))
-            spread_x(zz, yy)
-            return c
-        lax.fori_loop(0, NY - 1, body, 0)
-
-        def body_l(i, c):
-            wait_l(zz * NY + ypeer(i))
-            return c
-        lax.fori_loop(0, NY - 1, body_l, 0)
-        total = ldb[zz * NY]
-        for k in range(1, NY):
-            total = total + ldb[zz * NY + k]
-        ldg[zz * NX + x] = total
-
-        def body_g(i, c):
-            xl_copy(zz, i).start()
-            return c
-        lax.fori_loop(0, NX - 1, body_g, 0)
-
-    z_copy(0).start()
     z_copy(1).start()
-    spread_y(z)
-    spread_x(z, y)
+    spread_y(z, 1)
 
     for c in loads[4:]:
         c.wait()
@@ -228,11 +243,7 @@
         def body(i, c):
             xx = xpeer(i)
 
-            def arrive(k, c2):
-                wait_q(slot(zz, xx, k))
-                return c2
-
-            lax.fori_loop(0, NY, arrive, 0)
+            wait_row(zz, xx)
             wait_lg(zz * NX + xx)
             parts = adjoint(zz, xx)
             n = zz * (NX - 1) + i
@@ -244,7 +255,8 @@
 
     def r2_copy(zz, yy):
         n = zz * NY + yy
-        return remote(redb.at[n], rs2.at[own], s_r2.at[n], r_r2.at[own], dev(zz, x, yy))
+        n_to = jnp.where(zz == z, y, NY)
+        return remote(redb.at[n], rs2.at[own], s_r2.at[zz], r_r2.at[n_to], dev(zz, x, yy))
 
     def reduce_x(zz):
         for i in range(NX - 1):
@@ -254,18 +266,19 @@
             total = total + rs1[zz * (NX - 1) + i].reshape(BLK, COL).astype(jnp.float32)
         redb[pl.ds(zz * NY, NY)] = total.astype(jnp.bfloat16).reshape(NY, ROWS, COL)
 
-    pass_on(z)
-    wait_q(slot(zo, x, y))
+    rows_in(z, True)
+    wait_q(zo, y)
+    spread_y(zo, 0)
     wait_l(zo * NY + y)
-    spread_y(zo)
+    spread_y(zo, 1)
     spread_x(zo, y)
-    pass_on(zo)
     own_group(z)
+    rows_in(zo, True)
+    other_groups(z, 2, 3)
+    other_groups(z, 0, 2)
     own_group(zo)
-    other_groups(z, 0, 2)
+    other_groups(zo, 2, 3)
     other_groups(zo, 0, 2)
-    other_groups(z, 2, 3)
-    other_groups(zo, 2, 3)
     reduce_x(z)
 
     def near(i, c):
@@ -282,27 +295,35 @@
         return c
     lax.fori_loop(0, NY, far, 0)
 
+    z_copy(0).wait_send()
+    z_copy(1).wait_send()
+    for zz in range(NZ):
+        blocks = qg.at[pl.ds(0, NY - 1)]
+        remote(blocks, blocks, s_y.at[zz], r_q.at[0], dev(zo, x, y)).wait_send()
+        rows = ldb.at[pl.ds(0, NY - 1)]
+        remote(rows, rows, s_yl.at[zz], r_l.at[0], dev(zo, x, y)).wait_send()
+        for i in range(NX - 1):
+            row_copy(zz, i).wait_send()
+            xl_copy(zz, i).wait_send()
+            r1_copy(zz, i).wait_send()
+
     def landed_near(i, c):
         l = z * NY + ypeer(i)
-        remote(rs2.at[l], rs2.at[l], s_z.at[0], r_r2.at[l], dev(zo, x, y)).wait_recv()
+        remote(rs2.at[l], rs2.at[l], s_z.at[0], r_r2.at[ypeer(i)], dev(z, x, ypeer(i))).wait_recv()
         return c
     lax.fori_loop(0, NY - 1, landed_near, 0)
-
-    def landed_far(i, c):
-        l = zo * NY + i
-        remote(rs2.at[l], rs2.at[l], s_z.at[0], r_r2.at[l], dev(zo, x, y)).wait_recv()
-        return c
-    lax.fori_loop(0, NY, landed_far, 0)
+    far_part = rs2.at[pl.ds(zo * NY, NY)]
+    remote(far_part, far_part, s_z.at[0], r_r2.at[NY], dev(zo, x, y)).wait_recv()
 
     query_half = (jnp.sum(rs2[...].astype(jnp.float32), axis=0) * SCALE).astype(jnp.bfloat16)
     qg_out[...] = query_half
 
     def g_copy(j):
-        return remote(gs.at[j], gr.at[head], s_g.at[j], r_g.at[head], (obs, j))
+        return remote(gs.at[j], gr.at[head], s_g.at[0], r_g.at[head], (obs, j))
 
     parts = lax.dot_general(query_half, wb[...], (((1,), (1,)), ((), ())), preferred_element_type=jnp.float32)
     for j in range(HEADS):
-        gs[j] = parts[:, j * COL : (j + 1) * COL]
+        gs[j] = parts[:, j * COL : (j + 1) * COL].astype(jnp.bfloat16)
 
     def grid_send(i, c):
         g_copy((head + 1 + i) % HEADS).start()
@@ -310,49 +331,20 @@
     lax.fori_loop(0, HEADS - 1, grid_send, 0)
     gr[head] = gs[head]
 
+    near_part = redb.at[pl.ds(0, NY - 1)]
+    far_sent = redb.at[pl.ds(0, NY)]
+    remote(near_part, near_part, s_r2.at[z], r_r2.at[0], dev(zo, x, y)).wait_send()
+    remote(far_sent, far_sent, s_r2.at[zo], r_r2.at[0], dev(zo, x, y)).wait_send()
+
     def grid_landed(i, c):
         j = (head + 1 + i) % HEADS
-        remote(gr.at[j], gr.at[j], s_g.at[j], r_g.at[j], (obs, j)).wait_recv()
+        remote(gr.at[j], gr.at[j], s_g.at[0], r_g.at[j], (obs, j)).wait_recv()
         return c
     lax.fori_loop(0, HEADS - 1, grid_landed, 0)
-    gg_out[...] = jnp.sum(gr[...], axis=0).astype(jnp.bfloat16)
-
-    z_copy(0).wait_send()
-    z_copy(1).wait_send()
-
-    def sent_y(i, c):
-        for zz in (z, zo):
-            for copy in y_copies(zz, i):
-                copy.wait_send()
-        return c
-    lax.fori_loop(0, NY - 1, sent_y, 0)
-
-    def sent_x(i, c):
-        def inner(yy, c2):
-            x_copy(0, yy, i).wait_send()
-            x_copy(1, yy, i).wait_send()
-            return c2
-        lax.fori_loop(0, NY, inner, 0)
-        for zz in range(NZ):
-            xl_copy(zz, i).wait_send()
-            r1_copy(zz, i).wait_send()
-        return c
-    lax.fori_loop(0, NX - 1, sent_x, 0)
-
-    def sent_near(i, c):
-        r2_copy(z, ypeer(i)).wait_send()
-        return c
-    lax.fori_loop(0, NY - 1, sent_near, 0)
-
-    def sent_far(i, c):
-        r2_copy(zo, i).wait_send()
-        return c
-    lax.fori_loop(0, NY, sent_far, 0)
-
-    def sent_g(i, c):
-        g_copy((head + 1 + i) % HEADS).wait_send()
-        return c
-    lax.fori_loop(0, HEADS - 1, sent_g, 0)
+    gg_out[...] = jnp.sum(gr[...].astype(jnp.float32), axis=0).astype(jnp.bfloat16)
+
+    pieces = gs.at[pl.ds(0, HEADS - 1)]
+    remote(pieces, pieces, s_g.at[0], r_g.at[0], (obs, head)).wait_send()
 
 
 def finish(kob, vob, qgo, ggo, kg_hbm, vg_hbm, qg_hbm, gg_hbm, sem):
@@ -394,13 +386,12 @@
             pltpu.VMEM((NZ * (NX - 1), NY, ROWS, COL), bf),
             pltpu.VMEM((NZ * NY, ROWS, COL), bf),
             pltpu.VMEM((NZ * NY, ROWS, COL), bf),
-            pltpu.VMEM((HEADS, ROWS, COL), f32),
-            pltpu.VMEM((HEADS, ROWS, COL), f32),
-            dma((7,)), dma((2,)), dma((NZ * (NY - 1),)), dma((NZ * (NY - 1),)),
-            dma((NZ * NY * (NX - 1),)), dma((NZ * (NX - 1),)), dma((NZ * (NX - 1),)),
-            dma((NZ * NY,)), dma((HEADS,)),
-            dma((blocks,)), dma((NZ * NY,)), dma((NZ * NX,)), dma((NZ * (NX - 1),)),
-            dma((NZ * NY,)), dma((HEADS,)),
+            pltpu.VMEM((HEADS, ROWS, COL), bf),
+            pltpu.VMEM((HEADS, ROWS, COL), bf),
+            dma((7,)), dma((2,)), dma((NZ,)), dma((NZ,)), dma((NZ * (NX - 1),)), dma((NZ * (NX - 1),)),
+            dma((NZ * (NX - 1),)), dma((NZ,)), dma((1,)),
+            dma((NZ * NY,)), dma((NZ * NX,)), dma((NZ * NY,)), dma((NZ * NX,)), dma((NZ * (NX - 1),)),
+            dma((NY + 1,)), dma((HEADS,)),
         ],
         compiler_params=pltpu.CompilerParams(collective_id=0, has_side_effects=True),
     )(queries, out_grad, attn_out, logsumexp.T, keys, values, obs_counts, query_weight)

time: 55.6 us -> 53.2 us (0.957)
  Pallas kernels: 54.2 us -> 51.7 us
    pallas_call x1, Pallas kernels: 53.4 us -> 50.9 us  [on_device(): pl.pallas_call(kernel, name='adjoint', out_shape=tuple((pltpu.VMEM(shape,...]
where the time goes in v3:
time: 53.2 us; the launch traced here: 53 us
  Pallas kernels  51.7 us (97%)
  between operations  1.29 us (2%)
    pallas_call x1, Pallas kernels, on_device(): pl.pallas_call(kernel, name='adjoint', out_shape=tuple((pltpu.VMEM(shape,...  50.9 us

profile of v3, /device:TPU:1, one launch (start us, length us, event | category | flops | bytes accessed | tf_op | source)
XLA Modules:
  0.0 53.0 jit_solution(8757428958071607755)
XLA Ops:
  1.3 50.9 %adjoint.1 = (bf16[384,256]{1,0:T(8,128)(2,1)S(1)}, bf16[384,256]{1,0:T(8,128)(2,1)S(1)}, bf16[16,256]{1,0:T(8,128)(2,1)S(1)}, bf16[16,256]{1,0:T(8,128)(2,1)S(1)}) custom-call(bf16[16,256]{1,0:T(8,128)(2,1)} %q_hbm.1, bf16[16,256]{1,0:T(8,128)(2,1)} %g_hbm.1, bf16[16,256]{1,0:T(8,128)(2,1)} %o_hbm.1, f32[2,16]{1,0:T(2,128)} %bitcast.1, ...), custom_call_target="tpu_custom_call" | custom-call | tf_op jit(solution)/shard_map/adjoint/pallas_call | solution.py:366
  52.2 0.8 %finish.1 = (bf16[384,256]{1,0:T(8,128)(2,1)}, bf16[384,256]{1,0:T(8,128)(2,1)}, bf16[16,256]{1,0:T(8,128)(2,1)}, bf16[16,256]{1,0:T(8,128)(2,1)}) custom-call(bf16[384,256]{1,0:T(8,128)(2,1)S(1)} %get-tuple-element.8.kob, bf16[384,256]{1,0:T(8,128)(2,1)S(1)} %get-tuple-element.9.vob, bf16[16,256]{1,0:T(8,128)(2,1)S(1)} %get-tuple-element.10.qgo, ...), custom_call_target="tpu_custom_call" | custom-call | tf_op jit(solution)/shard_map/finish/pallas_call | solution.py:398

commit v4 on v3

--- a/solution.py
+++ b/solution.py
@@ -29,9 +29,9 @@
     q_hbm, g_hbm, o_hbm, lse_hbm, k_hbm, v_hbm, cnt, w_hbm,
     kob, vob, qg_out, gg_out,
     qg, att, lse_v, kb, vb, kt, wb,
-    ldb, ldg, dk, dv, dqs, dqo, rs1, redb, rs2, gs, gr,
-    sem_in, s_z, s_y, s_yl, s_x, s_xl, s_r1, s_r2, s_g,
-    r_q, r_x, r_l, r_lg, r_r1, r_r2, r_g,
+    ldb, ldg, pall, sall, dqs, dqo, rs1, redb, rs2, gs, gr,
+    sem_in, s_z, s_y, s_yl, s_x, s_f, s_xl, s_r1, s_r2, s_g,
+    r_q, r_x, r_f, r_l, r_lg, r_r1, r_r2, r_g,
 ):
     obs = lax.axis_index("obs")
     head = lax.axis_index("head")
@@ -148,24 +148,42 @@
             return c
         lax.fori_loop(0, NY - 1, body, 0)
 
-    def spread_x(zz, yy):
+    def spread_x(zz, yy, sides):
         def body(i, c):
             x_copy(zz, yy, i).start()
             return c
-        lax.fori_loop(0, NX - 1, body, 0)
-
-    def rows_in(zz, pieces):
+        lax.fori_loop(0, sides, body, 0)
+
+    xf = (x + NX // 2) % NX
+
+    def far_copy():
+        return remote(qg.at[me], qg.at[me], s_f.at[0], r_f.at[y], dev(z, xf, y))
+
+    def far_y_copy(i):
+        s = slot(z, xf, y)
+        return remote(qg.at[s], qg.at[s], s_f.at[1], r_f.at[y], dev(z, x, ypeer(i)))
+
+    def wait_far(yy):
+        s = slot(z, xf, yy)
+        remote(qg.at[s], qg.at[s], s_f.at[0], r_f.at[yy], dev(z, xf, y)).wait_recv()
+
+    def spread_far():
+        wait_far(y)
+
+        def body(i, c):
+            far_y_copy(i).start()
+            return c
+        lax.fori_loop(0, NY - 1, body, 0)
+
+    def rows_in(zz, sides, first, last):
         def body(i, c):
             yy = ypeer(i)
             wait_q(zz, yy)
-            if pieces:
-                spread_x(zz, yy)
-            return c
-        lax.fori_loop(0, NY - 1, body, 0)
-        if not pieces:
-            for i in range(NX - 1):
-                row_copy(zz, i).start()
-
+            spread_x(zz, yy, sides)
+            return c
+        lax.fori_loop(first, last, body, 0)
+
+    def rows_done(zz):
         def body_l(i, c):
             wait_l(zz * NY + ypeer(i))
             return c
@@ -182,7 +200,8 @@
 
     z_copy(0).start()
     spread_y(z, 0)
-    spread_x(z, y)
+    far_copy().start()
+    spread_x(z, y, 2)
 
     for c in loads[2:4]:
         c.wait()
@@ -206,12 +225,11 @@
         c.wait()
     for h in range(2):
         kt[h] = kb[:, h * DH : (h + 1) * DH].astype(jnp.float32).T.astype(jnp.bfloat16)
-    dk[...] = jnp.zeros_like(dk)
-    dv[...] = jnp.zeros_like(dv)
     live = lax.broadcasted_iota(jnp.int32, (TOK, BLK), 0) < cnt[0]
 
     def adjoint(zz, xx):
         base = slot(zz, xx, 0)
+        at = pl.ds(pl.multiple_of(base * ROWS, BLK), BLK)
         parts = []
         for h in range(2):
             cols = slice(h * DH, (h + 1) * DH)
@@ -224,8 +242,8 @@
             dprobs = lax.dot_general(vb[:, cols], gh, nt, preferred_element_type=jnp.float32)
             probs = jnp.where(live, jnp.exp2(scores * (SCALE * LOG2E) - lse), 0.0)
             dscores = (probs * (dprobs - delta)).astype(jnp.bfloat16)
-            dv[:, cols] += jnp.dot(probs.astype(jnp.bfloat16), gh, preferred_element_type=jnp.float32)
-            dk[:, cols] += jnp.dot(dscores, qh, preferred_element_type=jnp.float32)
+            pall[h, :, at] = probs.astype(jnp.bfloat16)
+            sall[h, :, at] = dscores
             dqt = jnp.dot(kt[h], dscores, preferred_element_type=jnp.float32)
             parts.append(dqt.T)
         return parts
@@ -243,7 +261,13 @@
         def body(i, c):
             xx = xpeer(i)
 
-            wait_row(zz, xx)
+            if zz is z and first == 2:
+                def arrive(k, c2):
+                    wait_far(ypeer(k))
+                    return c2
+                lax.fori_loop(0, NY - 1, arrive, 0)
+            else:
+                wait_row(zz, xx)
             wait_lg(zz * NX + xx)
             parts = adjoint(zz, xx)
             n = zz * (NX - 1) + i
@@ -266,16 +290,20 @@
             total = total + rs1[zz * (NX - 1) + i].reshape(BLK, COL).astype(jnp.float32)
         redb[pl.ds(zz * NY, NY)] = total.astype(jnp.bfloat16).reshape(NY, ROWS, COL)
 
-    rows_in(z, True)
+    rows_in(z, 2, 0, 4)
     wait_q(zo, y)
     spread_y(zo, 0)
     wait_l(zo * NY + y)
     spread_y(zo, 1)
-    spread_x(zo, y)
+    spread_x(zo, y, 3)
+    spread_far()
+    rows_in(z, 2, 4, NY - 1)
+    rows_done(z)
     own_group(z)
-    rows_in(zo, True)
+    rows_in(zo, 3, 0, NY - 1)
+    rows_done(zo)
+    other_groups(z, 0, 2)
     other_groups(z, 2, 3)
-    other_groups(z, 0, 2)
     own_group(zo)
     other_groups(zo, 2, 3)
     other_groups(zo, 0, 2)
@@ -286,8 +314,6 @@
         return c
     lax.fori_loop(0, NY - 1, near, 0)
     rs2[own] = redb[own]
-    kob[...] = (dk[...] * SCALE).astype(jnp.bfloat16)
-    vob[...] = dv[...].astype(jnp.bfloat16)
     reduce_x(zo)
 
     def far(i, c):
@@ -295,15 +321,27 @@
         return c
     lax.fori_loop(0, NY, far, 0)
 
+    for h in range(2):
+        cols = slice(h * DH, (h + 1) * DH)
+        all_q = qg[:, :, h * DH : (h + 1) * DH].reshape(NZ * NX * BLK, DH)
+        all_g = qg[:, :, COL + h * DH : COL + (h + 1) * DH].reshape(NZ * NX * BLK, DH)
+        key_sum = jnp.dot(sall[h], all_q, preferred_element_type=jnp.float32)
+        kob[:, cols] = (key_sum * SCALE).astype(jnp.bfloat16)
+        vob[:, cols] = jnp.dot(pall[h], all_g, preferred_element_type=jnp.float32).astype(jnp.bfloat16)
+
     z_copy(0).wait_send()
     z_copy(1).wait_send()
-    for zz in range(NZ):
-        blocks = qg.at[pl.ds(0, NY - 1)]
+    blocks = qg.at[pl.ds(0, NY - 1)]
+    rows = ldb.at[pl.ds(0, NY - 1)]
+    far_copy().wait_send()
+    remote(blocks, blocks, s_f.at[1], r_q.at[0], dev(zo, x, y)).wait_send()
+    row_copy(zo, 2).wait_send()
+    for zz in (z, zo):
         remote(blocks, blocks, s_y.at[zz], r_q.at[0], dev(zo, x, y)).wait_send()
-        rows = ldb.at[pl.ds(0, NY - 1)]
         remote(rows, rows, s_yl.at[zz], r_l.at[0], dev(zo, x, y)).wait_send()
+        row_copy(zz, 0).wait_send()
+        row_copy(zz, 1).wait_send()
         for i in range(NX - 1):
-            row_copy(zz, i).wait_send()
             xl_copy(zz, i).wait_send()
             r1_copy(zz, i).wait_send()
 
@@ -379,8 +417,8 @@
             pltpu.VMEM((HEADS * COL, COL), bf),
             pltpu.VMEM((NZ * NY, 4, BLK), f32),
             pltpu.VMEM((NZ * NX, 4, BLK), f32),
-            pltpu.VMEM((TOK, COL), f32),
-            pltpu.VMEM((TOK, COL), f32),
+            pltpu.VMEM((2, TOK, NZ * NX * BLK), bf),
+            pltpu.VMEM((2, TOK, NZ * NX * BLK), bf),
             pltpu.VMEM((NZ * (NX - 1), NY, ROWS, COL), bf),
             pltpu.VMEM((NZ, BLK, COL), f32),
             pltpu.VMEM((NZ * (NX - 1), NY, ROWS, COL), bf),
@@ -388,9 +426,9 @@
             pltpu.VMEM((NZ * NY, ROWS, COL), bf),
             pltpu.VMEM((HEADS, ROWS, COL), bf),
             pltpu.VMEM((HEADS, ROWS, COL), bf),
-            dma((7,)), dma((2,)), dma((NZ,)), dma((NZ,)), dma((NZ * (NX - 1),)), dma((NZ * (NX - 1),)),
+            dma((7,)), dma((2,)), dma((NZ,)), dma((NZ,)), dma((NZ * (NX - 1),)), dma((2,)), dma((NZ * (NX - 1),)),
             dma((NZ * (NX - 1),)), dma((NZ,)), dma((1,)),
-            dma((NZ * NY,)), dma((NZ * NX,)), dma((NZ * NY,)), dma((NZ * NX,)), dma((NZ * (NX - 1),)),
+            dma((NZ * NY,)), dma((NZ * NX,)), dma((NY,)), dma((NZ * NY,)), dma((NZ * NX,)), dma((NZ * (NX - 1),)),
             dma((NY + 1,)), dma((HEADS,)),
         ],
         compiler_params=pltpu.CompilerParams(collective_id=0, has_side_effects=True),

time: 53.2 us -> 51.9 us (0.976)
  Pallas kernels: 51.7 us -> 50.4 us
    pallas_call x1, Pallas kernels: 50.9 us -> 49.6 us  [on_device(): pl.pallas_call(kernel, name='adjoint', out_shape=tuple((pltpu.VMEM(shape,...]
where the time goes in v4:
time: 51.9 us; the launch traced here: 51.7 us
  Pallas kernels  50.4 us (97%)
  between operations  1.29 us (2%)
    pallas_call x1, Pallas kernels, on_device(): pl.pallas_call(kernel, name='adjoint', out_shape=tuple((pltpu.VMEM(shape,...  49.6 us

profile of v4, /device:TPU:1, one launch (start us, length us, event | category | flops | bytes accessed | tf_op | source)
XLA Modules:
  0.0 51.7 jit_solution(5292534026126350217)
XLA Ops:
  1.3 49.6 %adjoint.1 = (bf16[384,256]{1,0:T(8,128)(2,1)S(1)}, bf16[384,256]{1,0:T(8,128)(2,1)S(1)}, bf16[16,256]{1,0:T(8,128)(2,1)S(1)}, bf16[16,256]{1,0:T(8,128)(2,1)S(1)}) custom-call(bf16[16,256]{1,0:T(8,128)(2,1)} %q_hbm.1, bf16[16,256]{1,0:T(8,128)(2,1)} %g_hbm.1, bf16[16,256]{1,0:T(8,128)(2,1)} %o_hbm.1, f32[2,16]{1,0:T(2,128)} %bitcast.1, ...), custom_call_target="tpu_custom_call" | custom-call | tf_op jit(solution)/shard_map/adjoint/pallas_call | solution.py:404
  50.9 0.8 %finish.1 = (bf16[384,256]{1,0:T(8,128)(2,1)}, bf16[384,256]{1,0:T(8,128)(2,1)}, bf16[16,256]{1,0:T(8,128)(2,1)}, bf16[16,256]{1,0:T(8,128)(2,1)}) custom-call(bf16[384,256]{1,0:T(8,128)(2,1)S(1)} %get-tuple-element.8.kob, bf16[384,256]{1,0:T(8,128)(2,1)S(1)} %get-tuple-element.9.vob, bf16[16,256]{1,0:T(8,128)(2,1)S(1)} %get-tuple-element.10.qgo, ...), custom_call_target="tpu_custom_call" | custom-call | tf_op jit(solution)/shard_map/finish/pallas_call | solution.py:436

commit v5 on v4

--- a/solution.py
+++ b/solution.py
@@ -302,11 +302,11 @@
     own_group(z)
     rows_in(zo, 3, 0, NY - 1)
     rows_done(zo)
+    own_group(zo)
     other_groups(z, 0, 2)
     other_groups(z, 2, 3)
-    own_group(zo)
+    other_groups(zo, 0, 2)
     other_groups(zo, 2, 3)
-    other_groups(zo, 0, 2)
     reduce_x(z)
 
     def near(i, c):
@@ -317,7 +317,8 @@
     reduce_x(zo)
 
     def far(i, c):
-        r2_copy(zo, (y + i) % NY).start()
+        off = jnp.where(i == 0, NY // 2, NY // 2 + ring_offset(i - 1, NY))
+        r2_copy(zo, (y + off) % NY).start()
         return c
     lax.fori_loop(0, NY, far, 0)
 

time: 51.9 us -> 51.6 us (level)
  no operation moved by 1% of the time
where the time goes in v5:
time: 51.6 us; the launch traced here: 51.4 us
  Pallas kernels  50.1 us (97%)
  between operations  1.29 us (2%)
    pallas_call x1, Pallas kernels, on_device(): pl.pallas_call(kernel, name='adjoint', out_shape=tuple((pltpu.VMEM(shape,...  49.3 us

profile of v5, /device:TPU:1, one launch (start us, length us, event | category | flops | bytes accessed | tf_op | source)
XLA Modules:
  0.0 51.4 jit_solution(9788340435868288759)
XLA Ops:
  1.3 49.3 %adjoint.1 = (bf16[384,256]{1,0:T(8,128)(2,1)S(1)}, bf16[384,256]{1,0:T(8,128)(2,1)S(1)}, bf16[16,256]{1,0:T(8,128)(2,1)S(1)}, bf16[16,256]{1,0:T(8,128)(2,1)S(1)}) custom-call(bf16[16,256]{1,0:T(8,128)(2,1)} %q_hbm.1, bf16[16,256]{1,0:T(8,128)(2,1)} %g_hbm.1, bf16[16,256]{1,0:T(8,128)(2,1)} %o_hbm.1, f32[2,16]{1,0:T(2,128)} %bitcast.1, ...), custom_call_target="tpu_custom_call" | custom-call | tf_op jit(solution)/shard_map/adjoint/pallas_call | solution.py:405
  50.6 0.8 %finish.1 = (bf16[384,256]{1,0:T(8,128)(2,1)}, bf16[384,256]{1,0:T(8,128)(2,1)}, bf16[16,256]{1,0:T(8,128)(2,1)}, bf16[16,256]{1,0:T(8,128)(2,1)}) custom-call(bf16[384,256]{1,0:T(8,128)(2,1)S(1)} %get-tuple-element.8.kob, bf16[384,256]{1,0:T(8,128)(2,1)S(1)} %get-tuple-element.9.vob, bf16[16,256]{1,0:T(8,128)(2,1)S(1)} %get-tuple-element.10.qgo, ...), custom_call_target="tpu_custom_call" | custom-call | tf_op jit(solution)/shard_map/finish/pallas_call | solution.py:437

commit v6 on v5

--- a/solution.py
+++ b/solution.py
@@ -293,11 +293,11 @@
     rows_in(z, 2, 0, 4)
     wait_q(zo, y)
     spread_y(zo, 0)
+    spread_x(zo, y, 3)
+    rows_in(z, 2, 4, NY - 1)
     wait_l(zo * NY + y)
     spread_y(zo, 1)
-    spread_x(zo, y, 3)
     spread_far()
-    rows_in(z, 2, 4, NY - 1)
     rows_done(z)
     own_group(z)
     rows_in(zo, 3, 0, NY - 1)

time: 51.6 us -> 51.5 us (level)
  no operation moved by 1% of the time
where the time goes in v6:
time: 51.5 us; the launch traced here: 51.4 us
  Pallas kernels  50.1 us (97%)
  between operations  1.29 us (3%)
    pallas_call x1, Pallas kernels, on_device(): pl.pallas_call(kernel, name='adjoint', out_shape=tuple((pltpu.VMEM(shape,...  49.3 us

profile of v6, /device:TPU:1, one launch (start us, length us, event | category | flops | bytes accessed | tf_op | source)
XLA Modules:
  0.0 51.4 jit_solution(8625067341400026263)
XLA Ops:
  1.3 49.3 %adjoint.1 = (bf16[384,256]{1,0:T(8,128)(2,1)S(1)}, bf16[384,256]{1,0:T(8,128)(2,1)S(1)}, bf16[16,256]{1,0:T(8,128)(2,1)S(1)}, bf16[16,256]{1,0:T(8,128)(2,1)S(1)}) custom-call(bf16[16,256]{1,0:T(8,128)(2,1)} %q_hbm.1, bf16[16,256]{1,0:T(8,128)(2,1)} %g_hbm.1, bf16[16,256]{1,0:T(8,128)(2,1)} %o_hbm.1, f32[2,16]{1,0:T(2,128)} %bitcast.1, ...), custom_call_target="tpu_custom_call" | custom-call | tf_op jit(solution)/shard_map/adjoint/pallas_call | solution.py:405
  50.6 0.8 %finish.1 = (bf16[384,256]{1,0:T(8,128)(2,1)}, bf16[384,256]{1,0:T(8,128)(2,1)}, bf16[16,256]{1,0:T(8,128)(2,1)}, bf16[16,256]{1,0:T(8,128)(2,1)}) custom-call(bf16[384,256]{1,0:T(8,128)(2,1)S(1)} %get-tuple-element.8.kob, bf16[384,256]{1,0:T(8,128)(2,1)S(1)} %get-tuple-element.9.vob, bf16[16,256]{1,0:T(8,128)(2,1)S(1)} %get-tuple-element.10.qgo, ...), custom_call_target="tpu_custom_call" | custom-call | tf_op jit(solution)/shard_map/finish/pallas_call | solution.py:437
